TPU v7x, 32 devices: a whole 2x2x4 slice. The times are simulated.
32 devices in a mesh: row: 8 (over z, core), col: 4 (over y, x).
Axes of the slice: x: 2, y: 2, z: 4, core: 2. Of those that a mesh axis runs over, the one named last changes fastest.
Arguments:
- gradient: float32 [8192, 28672], P('row', 'col'), may hold values from -100 to 100
- residual: float32 [8192, 28672], P('row', 'col'), may hold values from -3 to 3
- q_init: float32 [4, 28672], P(None, 'col'), may hold values from -5 to 5
Outputs:
- q_factor: float32 [4, 28672], P(None, 'col')
- new_residual: float32 [8192, 28672], P('row', 'col')
All inputs are finite; a program needn't handle non-finite values.
Results may differ from a plain program's by a relative error of at most 0.00012.
Values sent between devices are 32-bit elements; how exact they have to be, the bound alone decides.
A program may use at most 128 MiB of HBM per device.

v0:
```python
import jax
import jax.numpy as jnp
from jax import lax
from jax.sharding import PartitionSpec as P

ITERS = 16


def sum_over_cols(partial_value):
    return lax.psum(partial_value, "col")


def shards(gradient, residual, q_init):
    highest = lax.Precision.HIGHEST
    merged = gradient + residual

    def iterate(step_index, carry):
        q_current, p_previous = carry
        p_partial = lax.dot_general(
            q_current,
            merged,
            (((1,), (1,)), ((), ())),
            precision=highest,
            preferred_element_type=jnp.float32,
        )
        p_factor = sum_over_cols(p_partial)
        gram_part = lax.dot_general(
            p_factor,
            p_factor,
            (((1,), (1,)), ((), ())),
            precision=highest,
            preferred_element_type=jnp.float32,
        )
        cross_part = jnp.dot(
            p_factor, merged, precision=highest, preferred_element_type=jnp.float32
        )
        gram, cross = lax.psum((gram_part, cross_part), "row")
        factor_low = jnp.linalg.cholesky(gram)
        p_basis = jax.scipy.linalg.solve_triangular(factor_low, p_factor, lower=True)
        q_next = jax.scipy.linalg.solve_triangular(factor_low, cross, lower=True)
        return (q_next, p_basis)

    start = (q_init, jnp.zeros((q_init.shape[0], merged.shape[0]), jnp.float32))
    q_factor, p_basis = lax.fori_loop(0, ITERS, iterate, start)
    approx = lax.dot_general(
        p_basis,
        q_factor,
        (((0,), (0,)), ((), ())),
        precision=highest,
        preferred_element_type=jnp.float32,
    )
    return (q_factor, merged - approx)


def solution(mesh):
    in_specs = (P("row", "col"), P("row", "col"), P(None, "col"))
    out_specs = (P(None, "col"), P("row", "col"))
    return jax.shard_map(shards, mesh=mesh, in_specs=in_specs, out_specs=out_specs, check_vma=False)
```

profile of v0, /device:TPU:1, one launch (start us, length us, event | category | flops | bytes accessed | tf_op | source)
XLA Modules:
  0.0 1912.1 jit_solution(13343573732617844287)
XLA Ops:
  7.2 30.9 %add.27 = f32[1024,7168]{1,0:T(8,128)} add(f32[1024,7168]{1,0:T(8,128)} %param.5, f32[1024,7168]{1,0:T(8,128)} %param.6) | non-fusion elementwise | flops 7340032 | bytes 88080384 | tf_op jit(solution)/shard_map/add | solution.py:15
  38.1 1837.0 %while.12 = (s32[]{:T(128)}, f32[4,7168]{1,0:T(4,128)S(1)}, f32[4,1024]{1,0:T(4,128)}, f32[1024,7168]{1,0:T(8,128)}, s32[]{:T(128)}) while((s32[]{:T(128)}, f32[4,7168]{1,0:T(4,128)S(1)}, f32[4,1024]{1,0:T(4,128)}, f32[1024,7168]{1,0:T(8,128)}, s32[]{:T(128)}) %tuple.27), condition=%wide.region_6.7_spmd, body=%wide.region_0.6_spmd.sunk | while | flops 706445440 | bytes 59982788 | solution.py:44
  38.1 27.1 %fusion.46 = f32[4,1024]{1,0:T(4,128)S(1)} fusion(f32[4,7168]{1,0:T(4,128)S(1)} %get-tuple-element.63, f32[1024,7168]{1,0:T(8,128)} %get-tuple-element.70), kind=kOutput, calls=%fused_computation.13.clone.1 | convolution fusion | flops 352321536 | bytes 29491200 | tf_op jit(solution)/shard_map/while/body/eval_jaxpr/dot_general | solution.py:19
  78.3 17.9 fusion.47
  117.1 35.7 %all-reduce.2.cloned.1.call-done = f32[4,7168]{1,0:T(4,128)} async-done(((f32[4,7168]{1,0:T(4,128)}), f32[4,7168]{1,0:T(4,128)}) %all-reduce.2.cloned.1.call-update) | async-done | bytes 114704 | tf_op jit(solution)/shard_map/while/body/eval_jaxpr/psum | solution.py:37
  154.1 27.1 %fusion.46 = f32[4,1024]{1,0:T(4,128)S(1)} fusion(f32[4,7168]{1,0:T(4,128)S(1)} %get-tuple-element.63, f32[1024,7168]{1,0:T(8,128)} %get-tuple-element.70), kind=kOutput, calls=%fused_computation.13.clone.1 | convolution fusion | flops 352321536 | bytes 29491200 | tf_op jit(solution)/shard_map/while/body/eval_jaxpr/dot_general | solution.py:19
  193.4 17.9 fusion.47
  231.7 35.8 %all-reduce.2.cloned.1.call-done = f32[4,7168]{1,0:T(4,128)} async-done(((f32[4,7168]{1,0:T(4,128)}), f32[4,7168]{1,0:T(4,128)}) %all-reduce.2.cloned.1.call-update) | async-done | bytes 114704 | tf_op jit(solution)/shard_map/while/body/eval_jaxpr/psum | solution.py:37
  268.9 27.1 %fusion.46 = f32[4,1024]{1,0:T(4,128)S(1)} fusion(f32[4,7168]{1,0:T(4,128)S(1)} %get-tuple-element.63, f32[1024,7168]{1,0:T(8,128)} %get-tuple-element.70), kind=kOutput, calls=%fused_computation.13.clone.1 | convolution fusion | flops 352321536 | bytes 29491200 | tf_op jit(solution)/shard_map/while/body/eval_jaxpr/dot_general | solution.py:19
  308.2 17.9 fusion.47
  346.5 35.8 %all-reduce.2.cloned.1.call-done = f32[4,7168]{1,0:T(4,128)} async-done(((f32[4,7168]{1,0:T(4,128)}), f32[4,7168]{1,0:T(4,128)}) %all-reduce.2.cloned.1.call-update) | async-done | bytes 114704 | tf_op jit(solution)/shard_map/while/body/eval_jaxpr/psum | solution.py:37
  383.7 27.1 %fusion.46 = f32[4,1024]{1,0:T(4,128)S(1)} fusion(f32[4,7168]{1,0:T(4,128)S(1)} %get-tuple-element.63, f32[1024,7168]{1,0:T(8,128)} %get-tuple-element.70), kind=kOutput, calls=%fused_computation.13.clone.1 | convolution fusion | flops 352321536 | bytes 29491200 | tf_op jit(solution)/shard_map/while/body/eval_jaxpr/dot_general | solution.py:19
  423.0 17.9 fusion.47
  461.3 35.8 %all-reduce.2.cloned.1.call-done = f32[4,7168]{1,0:T(4,128)} async-done(((f32[4,7168]{1,0:T(4,128)}), f32[4,7168]{1,0:T(4,128)}) %all-reduce.2.cloned.1.call-update) | async-done | bytes 114704 | tf_op jit(solution)/shard_map/while/body/eval_jaxpr/psum | solution.py:37
  498.4 27.1 %fusion.46 = f32[4,1024]{1,0:T(4,128)S(1)} fusion(f32[4,7168]{1,0:T(4,128)S(1)} %get-tuple-element.63, f32[1024,7168]{1,0:T(8,128)} %get-tuple-element.70), kind=kOutput, calls=%fused_computation.13.clone.1 | convolution fusion | flops 352321536 | bytes 29491200 | tf_op jit(solution)/shard_map/while/body/eval_jaxpr/dot_general | solution.py:19
  537.7 17.9 fusion.47
  576.0 35.8 %all-reduce.2.cloned.1.call-done = f32[4,7168]{1,0:T(4,128)} async-done(((f32[4,7168]{1,0:T(4,128)}), f32[4,7168]{1,0:T(4,128)}) %all-reduce.2.cloned.1.call-update) | async-done | bytes 114704 | tf_op jit(solution)/shard_map/while/body/eval_jaxpr/psum | solution.py:37
  613.1 27.1 %fusion.46 = f32[4,1024]{1,0:T(4,128)S(1)} fusion(f32[4,7168]{1,0:T(4,128)S(1)} %get-tuple-element.63, f32[1024,7168]{1,0:T(8,128)} %get-tuple-element.70), kind=kOutput, calls=%fused_computation.13.clone.1 | convolution fusion | flops 352321536 | bytes 29491200 | tf_op jit(solution)/shard_map/while/body/eval_jaxpr/dot_general | solution.py:19
  652.4 17.9 fusion.47
  690.7 35.8 %all-reduce.2.cloned.1.call-done = f32[4,7168]{1,0:T(4,128)} async-done(((f32[4,7168]{1,0:T(4,128)}), f32[4,7168]{1,0:T(4,128)}) %all-reduce.2.cloned.1.call-update) | async-done | bytes 114704 | tf_op jit(solution)/shard_map/while/body/eval_jaxpr/psum | solution.py:37
  727.9 27.1 %fusion.46 = f32[4,1024]{1,0:T(4,128)S(1)} fusion(f32[4,7168]{1,0:T(4,128)S(1)} %get-tuple-element.63, f32[1024,7168]{1,0:T(8,128)} %get-tuple-element.70), kind=kOutput, calls=%fused_computation.13.clone.1 | convolution fusion | flops 352321536 | bytes 29491200 | tf_op jit(solution)/shard_map/while/body/eval_jaxpr/dot_general | solution.py:19
  767.1 17.9 fusion.47
  805.4 35.8 %all-reduce.2.cloned.1.call-done = f32[4,7168]{1,0:T(4,128)} async-done(((f32[4,7168]{1,0:T(4,128)}), f32[4,7168]{1,0:T(4,128)}) %all-reduce.2.cloned.1.call-update) | async-done | bytes 114704 | tf_op jit(solution)/shard_map/while/body/eval_jaxpr/psum | solution.py:37
  842.6 27.1 %fusion.46 = f32[4,1024]{1,0:T(4,128)S(1)} fusion(f32[4,7168]{1,0:T(4,128)S(1)} %get-tuple-element.63, f32[1024,7168]{1,0:T(8,128)} %get-tuple-element.70), kind=kOutput, calls=%fused_computation.13.clone.1 | convolution fusion | flops 352321536 | bytes 29491200 | tf_op jit(solution)/shard_map/while/body/eval_jaxpr/dot_general | solution.py:19
  881.9 17.9 fusion.47
  920.2 35.8 %all-reduce.2.cloned.1.call-done = f32[4,7168]{1,0:T(4,128)} async-done(((f32[4,7168]{1,0:T(4,128)}), f32[4,7168]{1,0:T(4,128)}) %all-reduce.2.cloned.1.call-update) | async-done | bytes 114704 | tf_op jit(solution)/shard_map/while/body/eval_jaxpr/psum | solution.py:37
  957.3 27.1 %fusion.46 = f32[4,1024]{1,0:T(4,128)S(1)} fusion(f32[4,7168]{1,0:T(4,128)S(1)} %get-tuple-element.63, f32[1024,7168]{1,0:T(8,128)} %get-tuple-element.70), kind=kOutput, calls=%fused_computation.13.clone.1 | convolution fusion | flops 352321536 | bytes 29491200 | tf_op jit(solution)/shard_map/while/body/eval_jaxpr/dot_general | solution.py:19
  996.6 17.9 fusion.47
  1034.9 35.8 %all-reduce.2.cloned.1.call-done = f32[4,7168]{1,0:T(4,128)} async-done(((f32[4,7168]{1,0:T(4,128)}), f32[4,7168]{1,0:T(4,128)}) %all-reduce.2.cloned.1.call-update) | async-done | bytes 114704 | tf_op jit(solution)/shard_map/while/body/eval_jaxpr/psum | solution.py:37
  1072.1 27.1 %fusion.46 = f32[4,1024]{1,0:T(4,128)S(1)} fusion(f32[4,7168]{1,0:T(4,128)S(1)} %get-tuple-element.63, f32[1024,7168]{1,0:T(8,128)} %get-tuple-element.70), kind=kOutput, calls=%fused_computation.13.clone.1 | convolution fusion | flops 352321536 | bytes 29491200 | tf_op jit(solution)/shard_map/while/body/eval_jaxpr/dot_general | solution.py:19
  1111.4 17.9 fusion.47
  1149.7 35.8 %all-reduce.2.cloned.1.call-done = f32[4,7168]{1,0:T(4,128)} async-done(((f32[4,7168]{1,0:T(4,128)}), f32[4,7168]{1,0:T(4,128)}) %all-reduce.2.cloned.1.call-update) | async-done | bytes 114704 | tf_op jit(solution)/shard_map/while/body/eval_jaxpr/psum | solution.py:37
  1186.8 27.1 %fusion.46 = f32[4,1024]{1,0:T(4,128)S(1)} fusion(f32[4,7168]{1,0:T(4,128)S(1)} %get-tuple-element.63, f32[1024,7168]{1,0:T(8,128)} %get-tuple-element.70), kind=kOutput, calls=%fused_computation.13.clone.1 | convolution fusion | flops 352321536 | bytes 29491200 | tf_op jit(solution)/shard_map/while/body/eval_jaxpr/dot_general | solution.py:19
  1226.1 17.9 fusion.47
  1264.4 35.8 %all-reduce.2.cloned.1.call-done = f32[4,7168]{1,0:T(4,128)} async-done(((f32[4,7168]{1,0:T(4,128)}), f32[4,7168]{1,0:T(4,128)}) %all-reduce.2.cloned.1.call-update) | async-done | bytes 114704 | tf_op jit(solution)/shard_map/while/body/eval_jaxpr/psum | solution.py:37
  1301.5 27.1 %fusion.46 = f32[4,1024]{1,0:T(4,128)S(1)} fusion(f32[4,7168]{1,0:T(4,128)S(1)} %get-tuple-element.63, f32[1024,7168]{1,0:T(8,128)} %get-tuple-element.70), kind=kOutput, calls=%fused_computation.13.clone.1 | convolution fusion | flops 352321536 | bytes 29491200 | tf_op jit(solution)/shard_map/while/body/eval_jaxpr/dot_general | solution.py:19
  1340.8 17.9 fusion.47
  1379.1 35.8 %all-reduce.2.cloned.1.call-done = f32[4,7168]{1,0:T(4,128)} async-done(((f32[4,7168]{1,0:T(4,128)}), f32[4,7168]{1,0:T(4,128)}) %all-reduce.2.cloned.1.call-update) | async-done | bytes 114704 | tf_op jit(solution)/shard_map/while/body/eval_jaxpr/psum | solution.py:37
  1416.2 27.1 %fusion.46 = f32[4,1024]{1,0:T(4,128)S(1)} fusion(f32[4,7168]{1,0:T(4,128)S(1)} %get-tuple-element.63, f32[1024,7168]{1,0:T(8,128)} %get-tuple-element.70), kind=kOutput, calls=%fused_computation.13.clone.1 | convolution fusion | flops 352321536 | bytes 29491200 | tf_op jit(solution)/shard_map/while/body/eval_jaxpr/dot_general | solution.py:19
  1493.8 35.8 %all-reduce.2.cloned.1.call-done = f32[4,7168]{1,0:T(4,128)} async-done(((f32[4,7168]{1,0:T(4,128)}), f32[4,7168]{1,0:T(4,128)}) %all-reduce.2.cloned.1.call-update) | async-done | bytes 114704 | tf_op jit(solution)/shard_map/while/body/eval_jaxpr/psum | solution.py:37
  1531.0 27.1 %fusion.46 = f32[4,1024]{1,0:T(4,128)S(1)} fusion(f32[4,7168]{1,0:T(4,128)S(1)} %get-tuple-element.63, f32[1024,7168]{1,0:T(8,128)} %get-tuple-element.70), kind=kOutput, calls=%fused_computation.13.clone.1 | convolution fusion | flops 352321536 | bytes 29491200 | tf_op jit(solution)/shard_map/while/body/eval_jaxpr/dot_general | solution.py:19
  1608.6 35.8 %all-reduce.2.cloned.1.call-done = f32[4,7168]{1,0:T(4,128)} async-done(((f32[4,7168]{1,0:T(4,128)}), f32[4,7168]{1,0:T(4,128)}) %all-reduce.2.cloned.1.call-update) | async-done | bytes 114704 | tf_op jit(solution)/shard_map/while/body/eval_jaxpr/psum | solution.py:37
  1645.7 27.1 %fusion.46 = f32[4,1024]{1,0:T(4,128)S(1)} fusion(f32[4,7168]{1,0:T(4,128)S(1)} %get-tuple-element.63, f32[1024,7168]{1,0:T(8,128)} %get-tuple-element.70), kind=kOutput, calls=%fused_computation.13.clone.1 | convolution fusion | flops 352321536 | bytes 29491200 | tf_op jit(solution)/shard_map/while/body/eval_jaxpr/dot_general | solution.py:19
  1723.3 35.8 %all-reduce.2.cloned.1.call-done = f32[4,7168]{1,0:T(4,128)} async-done(((f32[4,7168]{1,0:T(4,128)}), f32[4,7168]{1,0:T(4,128)}) %all-reduce.2.cloned.1.call-update) | async-done | bytes 114704 | tf_op jit(solution)/shard_map/while/body/eval_jaxpr/psum | solution.py:37
  1760.5 27.1 %fusion.46 = f32[4,1024]{1,0:T(4,128)S(1)} fusion(f32[4,7168]{1,0:T(4,128)S(1)} %get-tuple-element.63, f32[1024,7168]{1,0:T(8,128)} %get-tuple-element.70), kind=kOutput, calls=%fused_computation.13.clone.1 | convolution fusion | flops 352321536 | bytes 29491200 | tf_op jit(solution)/shard_map/while/body/eval_jaxpr/dot_general | solution.py:19
  1799.7 17.9 fusion.47
  1838.0 35.8 %all-reduce.2.cloned.1.call-done = f32[4,7168]{1,0:T(4,128)} async-done(((f32[4,7168]{1,0:T(4,128)}), f32[4,7168]{1,0:T(4,128)}) %all-reduce.2.cloned.1.call-update) | async-done | bytes 114704 | tf_op jit(solution)/shard_map/while/body/eval_jaxpr/psum | solution.py:37
  1875.1 30.4 %convolution_subtract_fusion = f32[1024,7168]{1,0:T(8,128)} fusion(f32[1024,7168]{1,0:T(8,128)} %get-tuple-element.73, f32[4,1024]{1,0:T(4,128)} %get-tuple-element.25, f32[4,7168]{1,0:T(4,128)S(1)} %get-tuple-element.22), kind=kOutput, calls=%fused_computation.12 | convolution fusion | flops 359661568 | bytes 58851328 | tf_op jit(solution)/shard_map/dot_general | solution.py:45
  (232 shorter events, 597.8 us)
Async XLA Ops:
  7.2 31.0 %copy-start.1 = (f32[4,7168]{1,0:T(4,128)S(1)}, f32[4,7168]{1,0:T(4,128)}, u32[]{:S(2)}) copy-start(f32[4,7168]{1,0:T(4,128)} %param.7) | copy-start | bytes 344068
  38.1 114.7 %all-reduce.2.cloned.1.call-start = ((), (), s32[]{:S(2)}) async-start(), calls=%async_computation | async-start | bytes 229376 | tf_op jit(solution)/shard_map/while/body/eval_jaxpr/psum | solution.py:37
  154.1 113.5 %all-reduce.2.cloned.1.call-start = ((), (), s32[]{:S(2)}) async-start(), calls=%async_computation | async-start | bytes 229376 | tf_op jit(solution)/shard_map/while/body/eval_jaxpr/psum | solution.py:37
  268.9 113.4 %all-reduce.2.cloned.1.call-start = ((), (), s32[]{:S(2)}) async-start(), calls=%async_computation | async-start | bytes 229376 | tf_op jit(solution)/shard_map/while/body/eval_jaxpr/psum | solution.py:37
  383.6 113.4 %all-reduce.2.cloned.1.call-start = ((), (), s32[]{:S(2)}) async-start(), calls=%async_computation | async-start | bytes 229376 | tf_op jit(solution)/shard_map/while/body/eval_jaxpr/psum | solution.py:37
  498.3 113.4 %all-reduce.2.cloned.1.call-start = ((), (), s32[]{:S(2)}) async-start(), calls=%async_computation | async-start | bytes 229376 | tf_op jit(solution)/shard_map/while/body/eval_jaxpr/psum | solution.py:37
  613.1 113.4 %all-reduce.2.cloned.1.call-start = ((), (), s32[]{:S(2)}) async-start(), calls=%async_computation | async-start | bytes 229376 | tf_op jit(solution)/shard_map/while/body/eval_jaxpr/psum | solution.py:37
  727.8 113.4 %all-reduce.2.cloned.1.call-start = ((), (), s32[]{:S(2)}) async-start(), calls=%async_computation | async-start | bytes 229376 | tf_op jit(solution)/shard_map/while/body/eval_jaxpr/psum | solution.py:37
  842.5 113.4 %all-reduce.2.cloned.1.call-start = ((), (), s32[]{:S(2)}) async-start(), calls=%async_computation | async-start | bytes 229376 | tf_op jit(solution)/shard_map/while/body/eval_jaxpr/psum | solution.py:37
  957.3 113.4 %all-reduce.2.cloned.1.call-start = ((), (), s32[]{:S(2)}) async-start(), calls=%async_computation | async-start | bytes 229376 | tf_op jit(solution)/shard_map/while/body/eval_jaxpr/psum | solution.py:37
  1072.0 113.4 %all-reduce.2.cloned.1.call-start = ((), (), s32[]{:S(2)}) async-start(), calls=%async_computation | async-start | bytes 229376 | tf_op jit(solution)/shard_map/while/body/eval_jaxpr/psum | solution.py:37
  1186.7 113.4 %all-reduce.2.cloned.1.call-start = ((), (), s32[]{:S(2)}) async-start(), calls=%async_computation | async-start | bytes 229376 | tf_op jit(solution)/shard_map/while/body/eval_jaxpr/psum | solution.py:37
  1301.5 113.4 %all-reduce.2.cloned.1.call-start = ((), (), s32[]{:S(2)}) async-start(), calls=%async_computation | async-start | bytes 229376 | tf_op jit(solution)/shard_map/while/body/eval_jaxpr/psum | solution.py:37
  1416.2 113.4 %all-reduce.2.cloned.1.call-start = ((), (), s32[]{:S(2)}) async-start(), calls=%async_computation | async-start | bytes 229376 | tf_op jit(solution)/shard_map/while/body/eval_jaxpr/psum | solution.py:37
  1530.9 113.4 %all-reduce.2.cloned.1.call-start = ((), (), s32[]{:S(2)}) async-start(), calls=%async_computation | async-start | bytes 229376 | tf_op jit(solution)/shard_map/while/body/eval_jaxpr/psum | solution.py:37
  1645.7 113.4 %all-reduce.2.cloned.1.call-start = ((), (), s32[]{:S(2)}) async-start(), calls=%async_computation | async-start | bytes 229376 | tf_op jit(solution)/shard_map/while/body/eval_jaxpr/psum | solution.py:37
  1760.4 113.4 %all-reduce.2.cloned.1.call-start = ((), (), s32[]{:S(2)}) async-start(), calls=%async_computation | async-start | bytes 229376 | tf_op jit(solution)/shard_map/while/body/eval_jaxpr/psum | solution.py:37
  1875.1 30.4 %copy-start = (f32[4,7168]{1,0:T(4,128)}, f32[4,7168]{1,0:T(4,128)S(1)}, u32[]{:S(2)}) copy-start(f32[4,7168]{1,0:T(4,128)S(1)} %get-tuple-element.22) | copy-start | bytes 344068
Sparse Core Ops, SparseCore 0:
  96.4 56.3 all-reduce.1
  211.5 56.0 all-reduce.1
  326.3 55.9 all-reduce.1
  441.0 55.9 all-reduce.1
  555.7 55.9 all-reduce.1
  670.5 55.9 all-reduce.1
  785.2 55.9 all-reduce.1
  899.9 55.9 all-reduce.1
  1014.7 55.9 all-reduce.1
  1129.4 55.9 all-reduce.1
  1244.1 55.9 all-reduce.1
  1358.9 55.9 all-reduce.1
  1473.6 55.9 all-reduce.1
  1588.3 55.9 all-reduce.1
  1703.0 55.9 all-reduce.1
  1817.8 55.9 all-reduce.1
where the time goes:
time: 1910 us
  matrix products  786 us (41%)
  waiting for transfers between devices  573 us (30%)
  blocking collectives  471 us (25%)
  other arithmetic  65.4 us (3%)
    psum x16, waiting for transfers between devices, iterate(): gram, cross = lax.psum((gram_part, cross_part), 'row')  572 us
    dot_general x16, matrix products, iterate(): lax.dot_general(q_current, merged, (((1,), (1,)), ((), ())), precision=hi...  433 us
    dot_general x16, matrix products, iterate(): jnp.dot(p_factor, merged, precision=highest, preferred_element_type=jnp.f...  286 us
    psum x16, blocking collectives, iterate(): gram, cross = lax.psum((gram_part, cross_part), 'row')  274 us
    psum x16, blocking collectives, sum_over_cols(): return lax.psum(partial_value, 'col')  196 us
  transfers between devices with their start and end apart: 16, of which 16 were waited for; matrix products, arithmetic and copies ran while one was open for 3% of the time, Pallas kernels for 0%

commit v1 on v0

--- a/solution.py
+++ b/solution.py
@@ -7,7 +7,7 @@
 
 
 def sum_over_cols(partial_value):
-    return lax.psum(partial_value, "col")
+    return jnp.sum(lax.all_gather(partial_value, "col"), axis=0)
 
 
 def shards(gradient, residual, q_init):

time: 1910 us -> 1800 us (0.942)
  blocking collectives: 471 us -> 346 us
    psum x16 -> x0, blocking collectives: 196 us -> none  [sum_over_cols(): return lax.psum(partial_value, 'col')]
    all_gather x0 -> x16, blocking collectives: none -> 99.7 us  [sum_over_cols(): return jnp.sum(lax.all_gather(partial_value, 'col'), axis=0)]
    psum x16, blocking collectives: 274 us -> 246 us  [iterate(): gram, cross = lax.psum((gram_part, cross_part), 'row')]
where the time goes in v1:
time: 1800 us
  matrix products  787 us (44%)
  waiting for transfers between devices  587 us (33%)
  blocking collectives  346 us (19%)
  other arithmetic  65.7 us (4%)
    psum x16, waiting for transfers between devices, iterate(): gram, cross = lax.psum((gram_part, cross_part), 'row')  586 us
    dot_general x16, matrix products, iterate(): lax.dot_general(q_current, merged, (((1,), (1,)), ((), ())), precision=hi...  433 us
    dot_general x16, matrix products, iterate(): jnp.dot(p_factor, merged, precision=highest, preferred_element_type=jnp.f...  287 us
    psum x16, blocking collectives, iterate(): gram, cross = lax.psum((gram_part, cross_part), 'row')  246 us
    all_gather x16, blocking collectives, sum_over_cols(): return jnp.sum(lax.all_gather(partial_value, 'col'), axis=0)  99.7 us
  transfers between devices with their start and end apart: 16, of which 16 were waited for; matrix products, arithmetic and copies ran while one was open for 3% of the time, Pallas kernels for 0%

profile of v1, /device:TPU:1, one launch (start us, length us, event | category | flops | bytes accessed | tf_op | source)
XLA Modules:
  0.0 1801.9 jit_solution(8929783098629127069)
XLA Ops:
  7.2 30.9 %add.25 = f32[1024,7168]{1,0:T(8,128)} add(f32[1024,7168]{1,0:T(8,128)} %param.5, f32[1024,7168]{1,0:T(8,128)} %param.6) | non-fusion elementwise | flops 7340032 | bytes 88080384 | tf_op jit(solution)/shard_map/add | solution.py:15
  38.1 1726.8 %while.12 = (s32[]{:T(128)}, f32[4,7168]{1,0:T(4,128)S(1)}, f32[4,1024]{1,0:T(4,128)}, f32[1024,7168]{1,0:T(8,128)}, s32[]{:T(128)}, /*index=5*/f32[]{:T(128)}) while((s32[]{:T(128)}, f32[4,7168]{1,0:T(4,128)S(1)}, f32[4,1024]{1,0:T(4,128)}, f32[1024,7168]{1,0:T(8,128)}, s32[]{:T(128)}, /*index=5*/f32[]{:T(128)}) %tuple.27), condition=%wide.region_6.7_spmd, body=%wide.region_0.6_spmd.sunk | while | flops 706453632 | bytes 60113872 | solution.py:44
  38.1 27.1 %convolution_bitcast_fusion.2 = f32[1,4,1024]{2,1,0:T(4,128)S(1)} fusion(f32[4,7168]{1,0:T(4,128)S(1)} %get-tuple-element.64, f32[1024,7168]{1,0:T(8,128)} %get-tuple-element.72), kind=kOutput, calls=%fused_computation.clone.1 | convolution fusion | flops 352321536 | bytes 29491200 | tf_op jit(solution)/shard_map/while/body/eval_jaxpr/dot_general | solution.py:19
  72.3 17.9 fusion.44
  109.3 36.6 %all-reduce.2.cloned.1.call-done = f32[4,7168]{1,0:T(4,128)} async-done(((f32[4,7168]{1,0:T(4,128)}), f32[4,7168]{1,0:T(4,128)}) %all-reduce.2.cloned.1.call-update) | async-done | bytes 114704 | tf_op jit(solution)/shard_map/while/body/eval_jaxpr/psum | solution.py:37
  147.3 27.1 %convolution_bitcast_fusion.2 = f32[1,4,1024]{2,1,0:T(4,128)S(1)} fusion(f32[4,7168]{1,0:T(4,128)S(1)} %get-tuple-element.64, f32[1024,7168]{1,0:T(8,128)} %get-tuple-element.72), kind=kOutput, calls=%fused_computation.clone.1 | convolution fusion | flops 352321536 | bytes 29491200 | tf_op jit(solution)/shard_map/while/body/eval_jaxpr/dot_general | solution.py:19
  180.5 17.9 fusion.44
  217.1 36.6 %all-reduce.2.cloned.1.call-done = f32[4,7168]{1,0:T(4,128)} async-done(((f32[4,7168]{1,0:T(4,128)}), f32[4,7168]{1,0:T(4,128)}) %all-reduce.2.cloned.1.call-update) | async-done | bytes 114704 | tf_op jit(solution)/shard_map/while/body/eval_jaxpr/psum | solution.py:37
  255.1 27.1 %convolution_bitcast_fusion.2 = f32[1,4,1024]{2,1,0:T(4,128)S(1)} fusion(f32[4,7168]{1,0:T(4,128)S(1)} %get-tuple-element.64, f32[1024,7168]{1,0:T(8,128)} %get-tuple-element.72), kind=kOutput, calls=%fused_computation.clone.1 | convolution fusion | flops 352321536 | bytes 29491200 | tf_op jit(solution)/shard_map/while/body/eval_jaxpr/dot_general | solution.py:19
  288.4 17.9 fusion.44
  324.9 36.7 %all-reduce.2.cloned.1.call-done = f32[4,7168]{1,0:T(4,128)} async-done(((f32[4,7168]{1,0:T(4,128)}), f32[4,7168]{1,0:T(4,128)}) %all-reduce.2.cloned.1.call-update) | async-done | bytes 114704 | tf_op jit(solution)/shard_map/while/body/eval_jaxpr/psum | solution.py:37
  363.0 27.1 %convolution_bitcast_fusion.2 = f32[1,4,1024]{2,1,0:T(4,128)S(1)} fusion(f32[4,7168]{1,0:T(4,128)S(1)} %get-tuple-element.64, f32[1024,7168]{1,0:T(8,128)} %get-tuple-element.72), kind=kOutput, calls=%fused_computation.clone.1 | convolution fusion | flops 352321536 | bytes 29491200 | tf_op jit(solution)/shard_map/while/body/eval_jaxpr/dot_general | solution.py:19
  396.2 17.9 fusion.44
  432.8 36.7 %all-reduce.2.cloned.1.call-done = f32[4,7168]{1,0:T(4,128)} async-done(((f32[4,7168]{1,0:T(4,128)}), f32[4,7168]{1,0:T(4,128)}) %all-reduce.2.cloned.1.call-update) | async-done | bytes 114704 | tf_op jit(solution)/shard_map/while/body/eval_jaxpr/psum | solution.py:37
  470.8 27.1 %convolution_bitcast_fusion.2 = f32[1,4,1024]{2,1,0:T(4,128)S(1)} fusion(f32[4,7168]{1,0:T(4,128)S(1)} %get-tuple-element.64, f32[1024,7168]{1,0:T(8,128)} %get-tuple-element.72), kind=kOutput, calls=%fused_computation.clone.1 | convolution fusion | flops 352321536 | bytes 29491200 | tf_op jit(solution)/shard_map/while/body/eval_jaxpr/dot_general | solution.py:19
  504.1 17.9 fusion.44
  540.6 36.7 %all-reduce.2.cloned.1.call-done = f32[4,7168]{1,0:T(4,128)} async-done(((f32[4,7168]{1,0:T(4,128)}), f32[4,7168]{1,0:T(4,128)}) %all-reduce.2.cloned.1.call-update) | async-done | bytes 114704 | tf_op jit(solution)/shard_map/while/body/eval_jaxpr/psum | solution.py:37
  578.6 27.1 %convolution_bitcast_fusion.2 = f32[1,4,1024]{2,1,0:T(4,128)S(1)} fusion(f32[4,7168]{1,0:T(4,128)S(1)} %get-tuple-element.64, f32[1024,7168]{1,0:T(8,128)} %get-tuple-element.72), kind=kOutput, calls=%fused_computation.clone.1 | convolution fusion | flops 352321536 | bytes 29491200 | tf_op jit(solution)/shard_map/while/body/eval_jaxpr/dot_general | solution.py:19
  611.9 17.9 fusion.44
  648.5 36.7 %all-reduce.2.cloned.1.call-done = f32[4,7168]{1,0:T(4,128)} async-done(((f32[4,7168]{1,0:T(4,128)}), f32[4,7168]{1,0:T(4,128)}) %all-reduce.2.cloned.1.call-update) | async-done | bytes 114704 | tf_op jit(solution)/shard_map/while/body/eval_jaxpr/psum | solution.py:37
  686.5 27.1 %convolution_bitcast_fusion.2 = f32[1,4,1024]{2,1,0:T(4,128)S(1)} fusion(f32[4,7168]{1,0:T(4,128)S(1)} %get-tuple-element.64, f32[1024,7168]{1,0:T(8,128)} %get-tuple-element.72), kind=kOutput, calls=%fused_computation.clone.1 | convolution fusion | flops 352321536 | bytes 29491200 | tf_op jit(solution)/shard_map/while/body/eval_jaxpr/dot_general | solution.py:19
  719.8 17.9 fusion.44
  756.3 36.7 %all-reduce.2.cloned.1.call-done = f32[4,7168]{1,0:T(4,128)} async-done(((f32[4,7168]{1,0:T(4,128)}), f32[4,7168]{1,0:T(4,128)}) %all-reduce.2.cloned.1.call-update) | async-done | bytes 114704 | tf_op jit(solution)/shard_map/while/body/eval_jaxpr/psum | solution.py:37
  794.3 27.1 %convolution_bitcast_fusion.2 = f32[1,4,1024]{2,1,0:T(4,128)S(1)} fusion(f32[4,7168]{1,0:T(4,128)S(1)} %get-tuple-element.64, f32[1024,7168]{1,0:T(8,128)} %get-tuple-element.72), kind=kOutput, calls=%fused_computation.clone.1 | convolution fusion | flops 352321536 | bytes 29491200 | tf_op jit(solution)/shard_map/while/body/eval_jaxpr/dot_general | solution.py:19
  827.6 17.9 fusion.44
  864.2 36.7 %all-reduce.2.cloned.1.call-done = f32[4,7168]{1,0:T(4,128)} async-done(((f32[4,7168]{1,0:T(4,128)}), f32[4,7168]{1,0:T(4,128)}) %all-reduce.2.cloned.1.call-update) | async-done | bytes 114704 | tf_op jit(solution)/shard_map/while/body/eval_jaxpr/psum | solution.py:37
  902.2 27.1 %convolution_bitcast_fusion.2 = f32[1,4,1024]{2,1,0:T(4,128)S(1)} fusion(f32[4,7168]{1,0:T(4,128)S(1)} %get-tuple-element.64, f32[1024,7168]{1,0:T(8,128)} %get-tuple-element.72), kind=kOutput, calls=%fused_computation.clone.1 | convolution fusion | flops 352321536 | bytes 29491200 | tf_op jit(solution)/shard_map/while/body/eval_jaxpr/dot_general | solution.py:19
  935.5 17.9 fusion.44
  972.0 36.7 %all-reduce.2.cloned.1.call-done = f32[4,7168]{1,0:T(4,128)} async-done(((f32[4,7168]{1,0:T(4,128)}), f32[4,7168]{1,0:T(4,128)}) %all-reduce.2.cloned.1.call-update) | async-done | bytes 114704 | tf_op jit(solution)/shard_map/while/body/eval_jaxpr/psum | solution.py:37
  1010.0 27.1 %convolution_bitcast_fusion.2 = f32[1,4,1024]{2,1,0:T(4,128)S(1)} fusion(f32[4,7168]{1,0:T(4,128)S(1)} %get-tuple-element.64, f32[1024,7168]{1,0:T(8,128)} %get-tuple-element.72), kind=kOutput, calls=%fused_computation.clone.1 | convolution fusion | flops 352321536 | bytes 29491200 | tf_op jit(solution)/shard_map/while/body/eval_jaxpr/dot_general | solution.py:19
  1043.3 17.9 fusion.44
  1079.9 36.7 %all-reduce.2.cloned.1.call-done = f32[4,7168]{1,0:T(4,128)} async-done(((f32[4,7168]{1,0:T(4,128)}), f32[4,7168]{1,0:T(4,128)}) %all-reduce.2.cloned.1.call-update) | async-done | bytes 114704 | tf_op jit(solution)/shard_map/while/body/eval_jaxpr/psum | solution.py:37
  1117.9 27.1 %convolution_bitcast_fusion.2 = f32[1,4,1024]{2,1,0:T(4,128)S(1)} fusion(f32[4,7168]{1,0:T(4,128)S(1)} %get-tuple-element.64, f32[1024,7168]{1,0:T(8,128)} %get-tuple-element.72), kind=kOutput, calls=%fused_computation.clone.1 | convolution fusion | flops 352321536 | bytes 29491200 | tf_op jit(solution)/shard_map/while/body/eval_jaxpr/dot_general | solution.py:19
  1151.2 17.9 fusion.44
  1187.7 36.7 %all-reduce.2.cloned.1.call-done = f32[4,7168]{1,0:T(4,128)} async-done(((f32[4,7168]{1,0:T(4,128)}), f32[4,7168]{1,0:T(4,128)}) %all-reduce.2.cloned.1.call-update) | async-done | bytes 114704 | tf_op jit(solution)/shard_map/while/body/eval_jaxpr/psum | solution.py:37
  1225.7 27.1 %convolution_bitcast_fusion.2 = f32[1,4,1024]{2,1,0:T(4,128)S(1)} fusion(f32[4,7168]{1,0:T(4,128)S(1)} %get-tuple-element.64, f32[1024,7168]{1,0:T(8,128)} %get-tuple-element.72), kind=kOutput, calls=%fused_computation.clone.1 | convolution fusion | flops 352321536 | bytes 29491200 | tf_op jit(solution)/shard_map/while/body/eval_jaxpr/dot_general | solution.py:19
  1259.0 17.9 fusion.44
  1295.6 36.7 %all-reduce.2.cloned.1.call-done = f32[4,7168]{1,0:T(4,128)} async-done(((f32[4,7168]{1,0:T(4,128)}), f32[4,7168]{1,0:T(4,128)}) %all-reduce.2.cloned.1.call-update) | async-done | bytes 114704 | tf_op jit(solution)/shard_map/while/body/eval_jaxpr/psum | solution.py:37
  1333.6 27.1 %convolution_bitcast_fusion.2 = f32[1,4,1024]{2,1,0:T(4,128)S(1)} fusion(f32[4,7168]{1,0:T(4,128)S(1)} %get-tuple-element.64, f32[1024,7168]{1,0:T(8,128)} %get-tuple-element.72), kind=kOutput, calls=%fused_computation.clone.1 | convolution fusion | flops 352321536 | bytes 29491200 | tf_op jit(solution)/shard_map/while/body/eval_jaxpr/dot_general | solution.py:19
  1366.9 17.9 fusion.44
  1403.4 36.7 %all-reduce.2.cloned.1.call-done = f32[4,7168]{1,0:T(4,128)} async-done(((f32[4,7168]{1,0:T(4,128)}), f32[4,7168]{1,0:T(4,128)}) %all-reduce.2.cloned.1.call-update) | async-done | bytes 114704 | tf_op jit(solution)/shard_map/while/body/eval_jaxpr/psum | solution.py:37
  1441.4 27.1 %convolution_bitcast_fusion.2 = f32[1,4,1024]{2,1,0:T(4,128)S(1)} fusion(f32[4,7168]{1,0:T(4,128)S(1)} %get-tuple-element.64, f32[1024,7168]{1,0:T(8,128)} %get-tuple-element.72), kind=kOutput, calls=%fused_computation.clone.1 | convolution fusion | flops 352321536 | bytes 29491200 | tf_op jit(solution)/shard_map/while/body/eval_jaxpr/dot_general | solution.py:19
  1511.3 36.7 %all-reduce.2.cloned.1.call-done = f32[4,7168]{1,0:T(4,128)} async-done(((f32[4,7168]{1,0:T(4,128)}), f32[4,7168]{1,0:T(4,128)}) %all-reduce.2.cloned.1.call-update) | async-done | bytes 114704 | tf_op jit(solution)/shard_map/while/body/eval_jaxpr/psum | solution.py:37
  1549.3 27.1 %convolution_bitcast_fusion.2 = f32[1,4,1024]{2,1,0:T(4,128)S(1)} fusion(f32[4,7168]{1,0:T(4,128)S(1)} %get-tuple-element.64, f32[1024,7168]{1,0:T(8,128)} %get-tuple-element.72), kind=kOutput, calls=%fused_computation.clone.1 | convolution fusion | flops 352321536 | bytes 29491200 | tf_op jit(solution)/shard_map/while/body/eval_jaxpr/dot_general | solution.py:19
  1619.1 36.7 %all-reduce.2.cloned.1.call-done = f32[4,7168]{1,0:T(4,128)} async-done(((f32[4,7168]{1,0:T(4,128)}), f32[4,7168]{1,0:T(4,128)}) %all-reduce.2.cloned.1.call-update) | async-done | bytes 114704 | tf_op jit(solution)/shard_map/while/body/eval_jaxpr/psum | solution.py:37
  1657.1 27.1 %convolution_bitcast_fusion.2 = f32[1,4,1024]{2,1,0:T(4,128)S(1)} fusion(f32[4,7168]{1,0:T(4,128)S(1)} %get-tuple-element.64, f32[1024,7168]{1,0:T(8,128)} %get-tuple-element.72), kind=kOutput, calls=%fused_computation.clone.1 | convolution fusion | flops 352321536 | bytes 29491200 | tf_op jit(solution)/shard_map/while/body/eval_jaxpr/dot_general | solution.py:19
  1727.0 36.7 %all-reduce.2.cloned.1.call-done = f32[4,7168]{1,0:T(4,128)} async-done(((f32[4,7168]{1,0:T(4,128)}), f32[4,7168]{1,0:T(4,128)}) %all-reduce.2.cloned.1.call-update) | async-done | bytes 114704 | tf_op jit(solution)/shard_map/while/body/eval_jaxpr/psum | solution.py:37
  1764.9 30.4 %convolution_subtract_fusion = f32[1024,7168]{1,0:T(8,128)} fusion(f32[1024,7168]{1,0:T(8,128)} %get-tuple-element.76, f32[4,1024]{1,0:T(4,128)} %get-tuple-element.25, f32[4,7168]{1,0:T(4,128)S(1)} %get-tuple-element.22), kind=kOutput, calls=%fused_computation.13 | convolution fusion | flops 359661568 | bytes 58851328 | tf_op jit(solution)/shard_map/dot_general | solution.py:45
  (248 shorter events, 473.4 us)
Async XLA Ops:
  7.2 31.0 %copy-start.1 = (f32[4,7168]{1,0:T(4,128)S(1)}, f32[4,7168]{1,0:T(4,128)}, u32[]{:S(2)}) copy-start(f32[4,7168]{1,0:T(4,128)} %param.7) | copy-start | bytes 344068
  38.1 107.8 %all-reduce.2.cloned.1.call-start = ((), (), s32[]{:S(2)}) async-start(), calls=%async_computation | async-start | bytes 229376 | tf_op jit(solution)/shard_map/while/body/eval_jaxpr/psum | solution.py:37
  147.2 106.5 %all-reduce.2.cloned.1.call-start = ((), (), s32[]{:S(2)}) async-start(), calls=%async_computation | async-start | bytes 229376 | tf_op jit(solution)/shard_map/while/body/eval_jaxpr/psum | solution.py:37
  255.1 106.5 %all-reduce.2.cloned.1.call-start = ((), (), s32[]{:S(2)}) async-start(), calls=%async_computation | async-start | bytes 229376 | tf_op jit(solution)/shard_map/while/body/eval_jaxpr/psum | solution.py:37
  362.9 106.5 %all-reduce.2.cloned.1.call-start = ((), (), s32[]{:S(2)}) async-start(), calls=%async_computation | async-start | bytes 229376 | tf_op jit(solution)/shard_map/while/body/eval_jaxpr/psum | solution.py:37
  470.8 106.5 %all-reduce.2.cloned.1.call-start = ((), (), s32[]{:S(2)}) async-start(), calls=%async_computation | async-start | bytes 229376 | tf_op jit(solution)/shard_map/while/body/eval_jaxpr/psum | solution.py:37
  578.6 106.5 %all-reduce.2.cloned.1.call-start = ((), (), s32[]{:S(2)}) async-start(), calls=%async_computation | async-start | bytes 229376 | tf_op jit(solution)/shard_map/while/body/eval_jaxpr/psum | solution.py:37
  686.4 106.5 %all-reduce.2.cloned.1.call-start = ((), (), s32[]{:S(2)}) async-start(), calls=%async_computation | async-start | bytes 229376 | tf_op jit(solution)/shard_map/while/body/eval_jaxpr/psum | solution.py:37
  794.3 106.5 %all-reduce.2.cloned.1.call-start = ((), (), s32[]{:S(2)}) async-start(), calls=%async_computation | async-start | bytes 229376 | tf_op jit(solution)/shard_map/while/body/eval_jaxpr/psum | solution.py:37
  902.1 106.5 %all-reduce.2.cloned.1.call-start = ((), (), s32[]{:S(2)}) async-start(), calls=%async_computation | async-start | bytes 229376 | tf_op jit(solution)/shard_map/while/body/eval_jaxpr/psum | solution.py:37
  1010.0 106.5 %all-reduce.2.cloned.1.call-start = ((), (), s32[]{:S(2)}) async-start(), calls=%async_computation | async-start | bytes 229376 | tf_op jit(solution)/shard_map/while/body/eval_jaxpr/psum | solution.py:37
  1117.8 106.5 %all-reduce.2.cloned.1.call-start = ((), (), s32[]{:S(2)}) async-start(), calls=%async_computation | async-start | bytes 229376 | tf_op jit(solution)/shard_map/while/body/eval_jaxpr/psum | solution.py:37
  1225.7 106.5 %all-reduce.2.cloned.1.call-start = ((), (), s32[]{:S(2)}) async-start(), calls=%async_computation | async-start | bytes 229376 | tf_op jit(solution)/shard_map/while/body/eval_jaxpr/psum | solution.py:37
  1333.5 106.5 %all-reduce.2.cloned.1.call-start = ((), (), s32[]{:S(2)}) async-start(), calls=%async_computation | async-start | bytes 229376 | tf_op jit(solution)/shard_map/while/body/eval_jaxpr/psum | solution.py:37
  1441.4 106.5 %all-reduce.2.cloned.1.call-start = ((), (), s32[]{:S(2)}) async-start(), calls=%async_computation | async-start | bytes 229376 | tf_op jit(solution)/shard_map/while/body/eval_jaxpr/psum | solution.py:37
  1549.2 106.5 %all-reduce.2.cloned.1.call-start = ((), (), s32[]{:S(2)}) async-start(), calls=%async_computation | async-start | bytes 229376 | tf_op jit(solution)/shard_map/while/body/eval_jaxpr/psum | solution.py:37
  1657.1 106.5 %all-reduce.2.cloned.1.call-start = ((), (), s32[]{:S(2)}) async-start(), calls=%async_computation | async-start | bytes 229376 | tf_op jit(solution)/shard_map/while/body/eval_jaxpr/psum | solution.py:37
  1764.9 30.4 %copy-start = (f32[4,7168]{1,0:T(4,128)}, f32[4,7168]{1,0:T(4,128)S(1)}, u32[]{:S(2)}) copy-start(f32[4,7168]{1,0:T(4,128)S(1)} %get-tuple-element.22) | copy-start | bytes 344068
Sparse Core Ops, SparseCore 0:
  90.4 55.4 all-reduce.1
  198.6 55.1 all-reduce.1
  306.4 55.1 all-reduce.1
  414.3 55.1 all-reduce.1
  522.1 55.1 all-reduce.1
  630.0 55.1 all-reduce.1
  737.8 55.1 all-reduce.1
  845.7 55.1 all-reduce.1
  953.5 55.1 all-reduce.1
  1061.4 55.1 all-reduce.1
  1169.2 55.1 all-reduce.1
  1277.1 55.1 all-reduce.1
  1384.9 55.1 all-reduce.1
  1492.8 55.1 all-reduce.1
  1600.6 55.1 all-reduce.1
  1708.5 55.1 all-reduce.1
